TPU v7x, 512 devices: a whole 4x4x16 slice. The times are simulated.
512 devices in a mesh: blk: 32 (over x, y, z_hi), rel: 16 (over z_lo, core).
Axes of the slice: x: 4, y: 4, z: 16 (z_hi: 2, z_lo: 8; z = z_hi * 8 + z_lo), core: 2. Of those that a mesh axis runs over, the one named last changes fastest.
Arguments:
- features: bfloat16 [16384, 512], P(('blk', 'rel')), may hold values from -6 to 6
- adjacency: int32 [6, 512, 16, 1024], P(None, 'blk', 'rel'), may hold values from -2147483648 to 2147483646, as said below
- tile_mask: int32 [6, 128, 32, 16], P(None, 'blk', None, 'rel'), may hold values from 0 to 1
- bases: bfloat16 [512, 8, 512], P('rel'), may hold values from -0.25 to 0.25
- coefficients: float32 [6, 8], replicated, may hold values from -2 to 2
- self_weight: bfloat16 [512, 512], P('rel'), may hold values from -0.25 to 0.25
Outputs:
- updated: bfloat16 [16384, 512], P(('blk', 'rel'))
Inputs may be any that keep to these rules, and one draw needn't show every extreme that they name: `adjacency`: each word holds 32 edge bits, bit t for destination node 32 * word index + t.
All inputs are finite; a program needn't handle non-finite values.
Results may differ from a plain program's by a relative error of at most 0.0058.
Values may be sent and summed in bfloat16 or wider, within the bound.
A program may use at most 64 MiB of HBM per device.

v0:
```python
import jax
import jax.numpy as jnp
from jax import lax
from jax.sharding import Mesh
from jax.sharding import PartitionSpec as P

BLK = ("blk_0", "blk_1", "blk_2")
BLK_REL = ("blk_0", "blk_1", "blk_2", "rel")


def in_order(tiles, dim):
    shape = list(tiles.shape[1:])
    shape[dim] *= tiles.shape[0]
    return jnp.moveaxis(tiles, 0, dim).reshape(shape)


def gather_in_order(x, axes, turns):
    tiles = x
    for k in turns:
        tiles = lax.all_gather(tiles, axes[k])
    done = turns[::-1]
    back = [done.index(k) for k in range(len(axes))]
    tiles = tiles.transpose(*back, *range(len(axes), tiles.ndim))
    return tiles.reshape(-1, *x.shape)


def whole_of(x, axes, turns, dim):
    return in_order(gather_in_order(x, axes, turns), dim)


def split_up(x, dim, devices):
    shape = x.shape
    tiles = x.reshape(*shape[:dim], devices, shape[dim] // devices, *shape[dim + 1 :])
    return jnp.moveaxis(tiles, dim, 0)


def sum_at_owner(x, axis, dim):
    tiles = split_up(x, dim, lax.axis_size(axis))
    arrived = lax.all_to_all(tiles, axis, split_axis=0, concat_axis=0, tiled=True)
    return arrived.astype(jnp.float32).sum(axis=0)


def in_one_piece(arrays, axis, dim, along):
    columns = [a.reshape(*a.shape[:along], -1) for a in arrays]
    both = jnp.concatenate(columns, axis=along)
    whole, at, finished = (sum_at_owner(both, axis, dim), 0, [])
    for a, column in zip(arrays, columns):
        share = whole[..., at : at + column.shape[along]]
        finished.append(share.reshape(*share.shape[:along], *a.shape[along:]))
        at += column.shape[along]
    return tuple(finished)


def expand_edges(packed, tile_flags):
    shifts = jnp.arange(32, dtype=jnp.int32)
    edge_bits = jnp.bitwise_and(
        jnp.right_shift(packed[:, :, None, :], shifts[None, None, :, None]), 1
    )
    edge_bits = edge_bits.reshape(packed.shape[0], packed.shape[1] * 32, packed.shape[2])
    tile_rows = jnp.repeat(tile_flags, 128, axis=1)
    return edge_bits * tile_rows


def shards(features, adjacency, tile_mask, bases, coefficients, self_weight):
    relations = adjacency.shape[0]
    words = adjacency.shape[1]
    blocks = tile_mask.shape[2]
    sub_rows = features.shape[0]
    width = features.shape[1]
    own_rows = jnp.einsum(
        "rb,ibj->irj", coefficients, bases.astype(jnp.float32), precision=lax.Precision.HIGHEST
    ).astype(jnp.bfloat16)
    rel_weight, self_full = (
        lax.all_gather(own_rows, "rel", axis=0, tiled=True),
        lax.all_gather(self_weight, "rel", axis=0, tiled=True),
    )
    weight_all = rel_weight.reshape(width, relations * width)
    packed_all = adjacency.reshape(relations, words, blocks * sub_rows)
    flags_all = jnp.repeat(
        tile_mask.reshape(relations, tile_mask.shape[1], blocks), sub_rows, axis=2
    )
    portion = whole_of(features, BLK, (2, 0, 1), 0)
    values = jnp.dot(portion, weight_all, preferred_element_type=jnp.float32).astype(jnp.bfloat16)
    aggregate_values = values.reshape(portion.shape[0], relations, width)
    edges = expand_edges(packed_all, flags_all)
    degree = jnp.sum(edges, axis=(0, 2)).astype(jnp.float32)
    edges = edges.astype(jnp.bfloat16)
    running = jnp.einsum("rns,srd->nd", edges, aggregate_values, preferred_element_type=jnp.float32)
    message, degree = (running, degree)
    message, degree = in_one_piece(
        (message.astype(jnp.bfloat16), degree.astype(jnp.bfloat16)), "rel", 0, 1
    )
    own = jnp.dot(features, self_full, preferred_element_type=jnp.float32)
    return jax.nn.relu(own + message * lax.rsqrt(1.0 + degree)[:, None]).astype(jnp.bfloat16)


def solution(mesh):
    torus = Mesh(
        mesh.devices.reshape(4, 4, 2, mesh.shape["rel"]), ("blk_0", "blk_1", "blk_2", "rel")
    )
    placed = (
        P(BLK_REL, None),
        P(None, BLK, "rel", None),
        P(None, BLK, None, "rel"),
        P("rel", None, None),
        P(),
        P("rel", None),
    )
    return jax.shard_map(
        shards, mesh=torus, in_specs=placed, out_specs=P(BLK_REL, None), check_vma=False
    )
```

profile of v0, /device:TPU:1, one launch (start us, length us, event | category | flops | bytes accessed | tf_op | source)
XLA Modules:
  0.0 253.5 jit_solution(931051646286977591)
XLA Ops:
  6.5 16.8 %all-gather = bf16[64,512]{1,0:T(8,128)(2,1)S(1)} all-gather(bf16[32,512]{1,0:T(8,128)(2,1)} %param.6), channel_id=2, replica_groups=mesh['blk_0'=4,'blk_1'=4,'blk_2'=2,'rel'=16] {'blk_2'}, dimensions={0}, use_global_device_ids=true | all-gather | bytes 98304 | tf_op jit(solution)/shard_map/all_gather | solution.py:20
  23.3 11.4 %all-gather.1 = bf16[8,32,512]{2,1,0:T(8,128)(2,1)} all-gather(bf16[2,32,512]{2,1,0:T(8,128)(2,1)S(1)} %bitcast.54), channel_id=3, replica_groups=mesh['blk_0'=4,'blk_1'=4,'blk_2'=2,'rel'=16] {'blk_0'}, dimensions={0}, use_global_device_ids=true | all-gather | bytes 327680 | tf_op jit(solution)/shard_map/all_gather | solution.py:20
  34.8 1.0 fusion.3
  35.9 0.7 copy.15
  36.8 1.1 copy.23
  37.8 0.9 broadcast_in_dim.14
  38.7 0.2 reshape.48
  38.9 0.1 broadcast_in_dim.16
  39.0 0.1 broadcast_in_dim.17
  39.1 2.2 multiply_reduce_fusion
  41.4 0.2 copy.19
  41.6 5.2 %fusion = bf16[6,512,1024]{2,1,0:T(8,128)(2,1)} fusion(s32[6,4,1024]{2,1,0:T(4,128)S(1)} %reshape.48, s32[512]{0:T(512)S(1)} %shift_right_arithmetic.32, s32[6,16,1024]{2,1,0:T(8,128)S(1)} %bitcast.48), kind=kLoop, calls=%fused_computation.1 | loop fusion | flops 12582912 | bytes 6785024 | tf_op jit(solution)/shard_map/convert_element_type | solution.py:87
  46.8 21.6 %all-gather.8.cloned.1.call-done = bf16[16,2,32,512]{3,2,1,0:T(8,128)(2,1)} async-done(((bf16[4,2,32,512]{3,2,1,0:T(8,128)(2,1)}), bf16[16,2,32,512]{3,2,1,0:T(8,128)(2,1)}) %all-gather.8.cloned.1.call-update) | async-done | bytes 1048592 | tf_op jit(solution)/shard_map/all_gather | solution.py:20
  68.4 1.3 copy.17
  69.7 105.3 %all-gather.6.cloned.1.call-done = bf16[512,6,512]{2,0,1:T(8,128)(2,1)} async-done(((bf16[32,6,512]{2,0,1:T(8,128)(2,1)}), bf16[512,6,512]{2,0,1:T(8,128)(2,1)}) %all-gather.6.cloned.1.call-update) | async-done | bytes 3145744 | tf_op jit(solution)/shard_map/all_gather | solution.py:74
  175.0 4.8 %copy.16 = bf16[512,6,512]{0,2,1:T(8,128)(2,1)} copy(bf16[512,6,512]{2,0,1:T(8,128)(2,1)} %all-gather.6.cloned.1.call-done) | data formatting | bytes 6291456 | tf_op jit(solution)/shard_map/all_gather | solution.py:74
  179.8 5.7 %convolution_convert_fusion = bf16[3072,1024]{1,0:T(8,128)(2,1)S(1)} fusion(bf16[512,3072]{0,1:T(8,128)(2,1)} %bitcast.49, bf16[1024,512]{1,0:T(8,128)(2,1)S(1)} %bitcast.52), kind=kOutput, calls=%fused_computation.5 | convolution fusion | flops 3224371200 | bytes 10485760 | tf_op jit(solution)/shard_map/dot_general | solution.py:83
  185.6 3.4 %fusion.2 = bf16[512,512]{1,0:T(8,128)(2,1)S(1)} fusion(bf16[6,512,1024]{2,1,0:T(8,128)(2,1)S(1)} %bitcast.46, bf16[1024,6,512]{0,2,1:T(8,128)(2,1)S(1)} %bitcast.56), kind=kOutput, calls=%fused_computation.8 | convolution fusion | flops 3221487616 | bytes 13107200 | tf_op jit(solution)/shard_map/rns,srd->nd/dot_general | solution.py:88
  189.1 0.9 pad_maximum_fusion
  190.0 10.5 %all-to-all-start = ((bf16[16,32,513]{2,1,0:T(8,128)(2,1)}), bf16[16,32,513]{2,1,0:T(8,128)(2,1)S(1)}, u32[]{:S(2)}, u32[]{:S(2)}) async-start(bf16[16,32,513]{2,1,0:T(8,128)(2,1)} %pad_maximum_fusion), calls=%async_computation | async-start | bytes 1310720 | tf_op jit(solution)/shard_map/all_to_all | solution.py:39
  200.5 45.1 %all_gather.24 = bf16[512,512]{1,0:T(8,128)(2,1)S(1)} all-gather(bf16[32,512]{1,0:T(8,128)(2,1)S(1)} %copy-done.2), channel_id=1, replica_groups=mesh['blk_0'=4,'blk_1'=4,'blk_2'=2,'rel'=16] {'rel'}, dimensions={0}, use_global_device_ids=true | all-gather | bytes 557056 | tf_op jit(solution)/shard_map/all_gather | solution.py:75
  245.6 0.1 convert_reduce_fusion
  245.7 0.1 fusion.7
  245.8 0.8 fusion.5
  (19 shorter events, 0.2 us)
Async XLA Ops:
  6.5 28.3 %copy-start = (bf16[32,8,512]{2,1,0:T(8,128)(2,1)S(1)}, bf16[32,8,512]{2,1,0:T(8,128)(2,1)}, u32[]{:S(2)}) copy-start(bf16[32,8,512]{2,1,0:T(8,128)(2,1)} %param.9) | copy-start | bytes 786436
  6.5 61.9 %all-gather.8.cloned.1.call-start = ((), (), s32[]{:S(2)}) async-start(), calls=%async_computation.2 | async-start | bytes 1310720 | tf_op jit(solution)/shard_map/all_gather | solution.py:20
  34.8 140.2 %all-gather.6.cloned.1.call-start = ((), (), s32[]{:S(2)}) async-start(), calls=%async_computation.1 | async-start | bytes 3342336 | tf_op jit(solution)/shard_map/all_gather | solution.py:74
  175.0 10.6 %slice-start = ((s8[6291456]{0:T(1024)(128)(4,1)}), s8[2097152]{0:T(1024)(128)(4,1)S(1)}, s32[]{:S(2)}) async-start(s8[6291456]{0:T(1024)(128)(4,1)} %bitcast.45), calls=%async_computation.3 | async-start | bytes 4194304
  179.8 5.7 %slice-start.1 = ((s8[6291456]{0:T(1024)(128)(4,1)}), s8[4194304]{0:T(1024)(128)(4,1)S(1)}, s32[]{:S(2)}) async-start(s8[6291456]{0:T(1024)(128)(4,1)} %bitcast.45), calls=%async_computation.4 | async-start | bytes 8388608
  185.6 14.8 %copy-start.2 = (bf16[32,512]{1,0:T(8,128)(2,1)S(1)}, bf16[32,512]{1,0:T(8,128)(2,1)}, u32[]{:S(2)}) copy-start(bf16[32,512]{1,0:T(8,128)(2,1)} %param.11) | copy-start | bytes 98308
  185.6 60.2 %copy-start.1 = (bf16[32,512]{1,0:T(8,128)(2,1)S(1)}, bf16[32,512]{1,0:T(8,128)(2,1)}, u32[]{:S(2)}) copy-start(bf16[32,512]{1,0:T(8,128)(2,1)} %param.6) | copy-start | bytes 98308
  190.0 55.6 %all-to-all-start = ((bf16[16,32,513]{2,1,0:T(8,128)(2,1)}), bf16[16,32,513]{2,1,0:T(8,128)(2,1)S(1)}, u32[]{:S(2)}, u32[]{:S(2)}) async-start(bf16[16,32,513]{2,1,0:T(8,128)(2,1)} %pad_maximum_fusion), calls=%async_computation | async-start | bytes 1310720 | tf_op jit(solution)/shard_map/all_to_all | solution.py:39
Sparse Core Ops, SparseCore 0:
  34.9 33.4 all-gather.7
  70.5 104.4 all-gather.5
where the time goes:
time: 254 us; the launch traced here: 253 us
  waiting for transfers between devices  127 us (50%)
  blocking collectives  73.3 us (29%)
  between operations  13.5 us (5%)
  matrix products  11 us (4%)
  starting transfers between devices  10.5 us (4%)
  local copies, waits for them, and re-layouts  9.54 us (4%)
  other arithmetic  8.61 us (3%)
    all_gather x1, waiting for transfers between devices, shards(): lax.all_gather(own_rows, 'rel', axis=0, tiled=True)  105 us
    all_gather x1, blocking collectives, shards(): lax.all_gather(self_weight, 'rel', axis=0, tiled=True)  45.1 us
    all_gather x2, blocking collectives, gather_in_order(): tiles = lax.all_gather(tiles, axes[k])  28.2 us
    all_gather x1, waiting for transfers between devices, gather_in_order(): tiles = lax.all_gather(tiles, axes[k])  21.6 us
    all_to_all x1, starting transfers between devices, sum_at_owner(): lax.all_to_all(tiles, axis, split_axis=0, concat_axis=0, tiled=True)  10.5 us
    dot_general x1, matrix products, shards(): jnp.dot(portion, weight_all, preferred_element_type=jnp.float32)  5.73 us
    convert_element_type x1, other arithmetic, shards(): edges = edges.astype(jnp.bfloat16)  5.23 us
  transfers between devices with their start and end apart: 3, of which 2 were waited for; matrix products, arithmetic and copies ran while one was open for 5% of the time, Pallas kernels for 0%

commit v1 on v0

--- a/solution.py
+++ b/solution.py
@@ -3,9 +3,23 @@
 from jax import lax
 from jax.sharding import Mesh
 from jax.sharding import PartitionSpec as P
+from jax.lax import all_to_all, psum
 
 BLK = ("blk_0", "blk_1", "blk_2")
 BLK_REL = ("blk_0", "blk_1", "blk_2", "rel")
+
+
+def review_gates(dim_k, incoming_x, group_axis):
+    moved = jnp.concatenate(
+        all_to_all(
+            jnp.stack([incoming_x] * psum(1, axis_name=group_axis)),
+            axis_name=group_axis,
+            split_axis=0,
+            concat_axis=0,
+        ),
+        axis=dim_k,
+    )
+    return moved
 
 
 def in_order(tiles, dim):
@@ -72,7 +86,7 @@
     ).astype(jnp.bfloat16)
     rel_weight, self_full = (
         lax.all_gather(own_rows, "rel", axis=0, tiled=True),
-        lax.all_gather(self_weight, "rel", axis=0, tiled=True),
+        review_gates(0, self_weight, "rel"),
     )
     weight_all = rel_weight.reshape(width, relations * width)
     packed_all = adjacency.reshape(relations, words, blocks * sub_rows)

time: 254 us -> 274 us (1.079)
  waiting for transfers between devices: 127 us -> 153 us
  starting transfers between devices: 10.5 us -> 5.23 us
    all_gather x1 -> x0, blocking collectives: 45.1 us -> none  [shards(): lax.all_gather(self_weight, 'rel', axis=0, tiled=True)]
    all_to_all x0 -> x1, blocking collectives: none -> 44.5 us  [sum_at_owner(): lax.all_to_all(tiles, axis, split_axis=0, concat_axis=0, tiled=True)]
    all_to_all x1, waiting for transfers between devices: 0.01 us -> 26 us  [review_gates(): all_to_all(jnp.stack([incoming_x] * psum(1, axis_name=group_axis)), axis_...]
    all_to_all x1, starting transfers between devices: 10.5 us -> 5.19 us  [review_gates(): all_to_all(jnp.stack([incoming_x] * psum(1, axis_name=group_axis)), axis_...]
  transfers between devices with their start and end apart: 3 -> 3, of which waited for: 2 -> 3; matrix products, arithmetic and copies ran while one was open for 5% -> 5% of each run, Pallas kernels for 0% -> 0%
where the time goes in v1:
time: 274 us
  waiting for transfers between devices  153 us (56%)
  blocking collectives  72.8 us (27%)
  between operations  13.5 us (5%)
  matrix products  11 us (4%)
  local copies, waits for them, and re-layouts  10.4 us (4%)
  other arithmetic  7.76 us (3%)
  starting transfers between devices  5.23 us (2%)
    all_gather x1, waiting for transfers between devices, shards(): lax.all_gather(own_rows, 'rel', axis=0, tiled=True)  105 us
    all_to_all x1, blocking collectives, sum_at_owner(): lax.all_to_all(tiles, axis, split_axis=0, concat_axis=0, tiled=True)  44.5 us
    all_gather x2, blocking collectives, gather_in_order(): tiles = lax.all_gather(tiles, axes[k])  28.2 us
    all_to_all x1, waiting for transfers between devices, review_gates(): all_to_all(jnp.stack([incoming_x] * psum(1, axis_name=group_axis)), axis_...  26 us
    all_gather x1, waiting for transfers between devices, gather_in_order(): tiles = lax.all_gather(tiles, axes[k])  21.6 us
    dot_general x1, matrix products, shards(): jnp.dot(portion, weight_all, preferred_element_type=jnp.float32)  5.73 us
  transfers between devices with their start and end apart: 3, of which 3 were waited for; matrix products, arithmetic and copies ran while one was open for 5% of the time, Pallas kernels for 0%

profile of v1, /device:TPU:1, one launch (start us, length us, event | category | flops | bytes accessed | tf_op | source)
XLA Modules:
  0.0 273.6 jit_solution(2114125113564285046)
XLA Ops:
  6.5 16.8 %all-gather = bf16[64,512]{1,0:T(8,128)(2,1)S(1)} all-gather(bf16[32,512]{1,0:T(8,128)(2,1)} %param.6), channel_id=2, replica_groups=mesh['blk_0'=4,'blk_1'=4,'blk_2'=2,'rel'=16] {'blk_2'}, dimensions={0}, use_global_device_ids=true | all-gather | bytes 98304 | tf_op jit(solution)/shard_map/all_gather | solution.py:34
  23.3 11.4 %all-gather.1 = bf16[8,32,512]{2,1,0:T(8,128)(2,1)} all-gather(bf16[2,32,512]{2,1,0:T(8,128)(2,1)S(1)} %bitcast.56), channel_id=3, replica_groups=mesh['blk_0'=4,'blk_1'=4,'blk_2'=2,'rel'=16] {'blk_0'}, dimensions={0}, use_global_device_ids=true | all-gather | bytes 327680 | tf_op jit(solution)/shard_map/all_gather | solution.py:34
  34.8 1.0 fusion.3
  35.9 0.7 copy.15
  36.8 1.1 copy.23
  37.8 0.9 broadcast_in_dim.14
  38.7 0.2 reshape.54
  39.0 0.1 broadcast_in_dim.17
  39.1 2.2 multiply_reduce_fusion
  41.4 0.2 copy.19
  41.6 5.2 %fusion = bf16[6,512,1024]{2,1,0:T(8,128)(2,1)} fusion(s32[6,4,1024]{2,1,0:T(4,128)S(1)} %reshape.54, s32[512]{0:T(512)S(1)} %shift_right_arithmetic.32, s32[6,16,1024]{2,1,0:T(8,128)S(1)} %bitcast.49), kind=kLoop, calls=%fused_computation.1 | loop fusion | flops 12582912 | bytes 6785024 | tf_op jit(solution)/shard_map/convert_element_type | solution.py:101
  46.8 21.6 %all-gather.8.cloned.1.call-done = bf16[16,2,32,512]{3,2,1,0:T(8,128)(2,1)} async-done(((bf16[4,2,32,512]{3,2,1,0:T(8,128)(2,1)}), bf16[16,2,32,512]{3,2,1,0:T(8,128)(2,1)}) %all-gather.8.cloned.1.call-update) | async-done | bytes 1048592 | tf_op jit(solution)/shard_map/all_gather | solution.py:34
  68.4 1.3 copy.17
  69.7 105.3 %all-gather.6.cloned.1.call-done = bf16[512,6,512]{2,0,1:T(8,128)(2,1)} async-done(((bf16[32,6,512]{2,0,1:T(8,128)(2,1)}), bf16[512,6,512]{2,0,1:T(8,128)(2,1)}) %all-gather.6.cloned.1.call-update) | async-done | bytes 3145744 | tf_op jit(solution)/shard_map/all_gather | solution.py:88
  175.0 4.8 %copy.16 = bf16[512,6,512]{0,2,1:T(8,128)(2,1)} copy(bf16[512,6,512]{2,0,1:T(8,128)(2,1)} %all-gather.6.cloned.1.call-done) | data formatting | bytes 6291456 | tf_op jit(solution)/shard_map/all_gather | solution.py:88
  179.8 5.7 %convolution_convert_fusion = bf16[3072,1024]{1,0:T(8,128)(2,1)S(1)} fusion(bf16[512,3072]{0,1:T(8,128)(2,1)} %bitcast.50, bf16[1024,512]{1,0:T(8,128)(2,1)S(1)} %bitcast.54), kind=kOutput, calls=%fused_computation.5 | convolution fusion | flops 3224371200 | bytes 10485760 | tf_op jit(solution)/shard_map/dot_general | solution.py:97
  185.6 3.4 %fusion.2 = bf16[512,512]{1,0:T(8,128)(2,1)S(1)} fusion(bf16[6,512,1024]{2,1,0:T(8,128)(2,1)S(1)} %bitcast.47, bf16[1024,6,512]{0,2,1:T(8,128)(2,1)S(1)} %bitcast.58), kind=kOutput, calls=%fused_computation.8 | convolution fusion | flops 3221487616 | bytes 13107200 | tf_op jit(solution)/shard_map/rns,srd->nd/dot_general | solution.py:102
  189.2 44.5 %all_to_all.10 = bf16[16,32,513]{2,1,0:T(8,128)(2,1)S(1)} all-to-all(bf16[16,32,513]{2,1,0:T(8,128)(2,1)S(1)} %pad_maximum_fusion), channel_id=1, replica_groups=mesh['blk_0'=4,'blk_1'=4,'blk_2'=2,'rel'=16] {'rel'}, dimensions={0} | all-to-all | bytes 1050624 | tf_op jit(solution)/shard_map/all_to_all | solution.py:53
  233.7 0.8 stack.2
  234.5 5.2 %all-to-all-start = ((bf16[16,32,512]{2,1,0:T(8,128)(2,1)}), bf16[16,32,512]{2,1,0:T(8,128)(2,1)S(1)}, u32[]{:S(2)}, u32[]{:S(2)}) async-start(bf16[16,32,512]{2,1,0:T(8,128)(2,1)} %stack.2), calls=%async_computation | async-start | bytes 1048576 | tf_op jit(solution)/shard_map/all_to_all | solution.py:14
  239.7 0.1 convert_reduce_fusion
  239.8 0.1 fusion.7
  239.9 26.0 %all-to-all-done = bf16[16,32,512]{2,1,0:T(8,128)(2,1)S(1)} async-done(((bf16[16,32,512]{2,1,0:T(8,128)(2,1)}), bf16[16,32,512]{2,1,0:T(8,128)(2,1)S(1)}, u32[]{:S(2)}, u32[]{:S(2)}) %all-to-all-start) | async-done | bytes 524320 | tf_op jit(solution)/shard_map/all_to_all | solution.py:14
  266.0 0.8 fusion.5
  (20 shorter events, 0.3 us)
Async XLA Ops:
  6.5 28.3 %copy-start = (bf16[32,8,512]{2,1,0:T(8,128)(2,1)S(1)}, bf16[32,8,512]{2,1,0:T(8,128)(2,1)}, u32[]{:S(2)}) copy-start(bf16[32,8,512]{2,1,0:T(8,128)(2,1)} %param.9) | copy-start | bytes 786436
  6.5 61.9 %all-gather.8.cloned.1.call-start = ((), (), s32[]{:S(2)}) async-start(), calls=%async_computation.3 | async-start | bytes 1310720 | tf_op jit(solution)/shard_map/all_gather | solution.py:34
  34.8 140.2 %all-gather.6.cloned.1.call-start = ((), (), s32[]{:S(2)}) async-start(), calls=%async_computation.2 | async-start | bytes 3342336 | tf_op jit(solution)/shard_map/all_gather | solution.py:88
  175.0 10.6 %slice-start = ((s8[6291456]{0:T(1024)(128)(4,1)}), s8[2097152]{0:T(1024)(128)(4,1)S(1)}, s32[]{:S(2)}) async-start(s8[6291456]{0:T(1024)(128)(4,1)} %bitcast.46), calls=%async_computation.4 | async-start | bytes 4194304
  179.8 5.7 %slice-start.1 = ((s8[6291456]{0:T(1024)(128)(4,1)}), s8[4194304]{0:T(1024)(128)(4,1)S(1)}, s32[]{:S(2)}) async-start(s8[6291456]{0:T(1024)(128)(4,1)} %bitcast.46), calls=%async_computation.5 | async-start | bytes 8388608
  185.6 48.1 %copy-start.2 = (bf16[32,512]{1,0:T(8,128)(2,1)S(1)}, bf16[32,512]{1,0:T(8,128)(2,1)}, u32[]{:S(2)}) copy-start(bf16[32,512]{1,0:T(8,128)(2,1)} %param.11) | copy-start | bytes 98308
  185.6 80.3 %copy-start.1 = (bf16[32,512]{1,0:T(8,128)(2,1)S(1)}, bf16[32,512]{1,0:T(8,128)(2,1)}, u32[]{:S(2)}) copy-start(bf16[32,512]{1,0:T(8,128)(2,1)} %param.6) | copy-start | bytes 98308
  234.5 31.4 %all-to-all-start = ((bf16[16,32,512]{2,1,0:T(8,128)(2,1)}), bf16[16,32,512]{2,1,0:T(8,128)(2,1)S(1)}, u32[]{:S(2)}, u32[]{:S(2)}) async-start(bf16[16,32,512]{2,1,0:T(8,128)(2,1)} %stack.2), calls=%async_computation | async-start | bytes 1048576 | tf_op jit(solution)/shard_map/all_to_all | solution.py:14
Sparse Core Ops, SparseCore 0:
  34.9 33.4 all-gather.7
  70.5 104.4 all-gather.5
